TPU v7x, 32 devices: a whole 2x2x4 slice. The times are simulated.
32 devices in a mesh: rep: 8 (over z, core), tp: 4 (over y, x).
Axes of the slice: x: 2, y: 2, z: 4, core: 2. Of those that a mesh axis runs over, the one named last changes fastest.
Arguments:
- queries: bfloat16 [64, 8192], P('rep', 'tp'), may hold values from -200 to 200
- new_keys: bfloat16 [64, 1024], P('rep', 'tp'), may hold values from -6 to 6
- new_values: bfloat16 [64, 1024], P('rep', 'tp'), may hold values from -6 to 6
- key_pool: bfloat16 [768, 128, 1024], P('rep', 'tp'), may hold values from -6 to 6
- value_pool: bfloat16 [768, 128, 1024], P('rep', 'tp'), may hold values from -6 to 6
- lengths: int32 [64], replicated, may hold values from 1 to 1536, as said below
- page_table: int32 [64, 12], P('rep'), may hold values from -1 to 95, as said below
- mig_slot: int32 [8], replicated, may hold values from 0 to 7
- mig_dst: int32 [8], replicated, may hold values from 0 to 7, as said below
Outputs:
- attended: bfloat16 [64, 8192], P('rep', 'tp')
- moved_keys: bfloat16 [96, 128, 1024], P('rep', 'tp')
- moved_values: bfloat16 [96, 128, 1024], P('rep', 'tp')
Inputs may be any that keep to these rules, and one draw needn't show every extreme that they name: mig_dst[r] = (r + c) mod 8 for one offset c with 1 <= c < 8, the same for every replica. `page_table`: row q lists distinct pool pages of its replica for its first ceil(lengths[q] / 128) pages and -1 after them. `lengths`: some request has exactly 1536 cached tokens.
All inputs are finite; a program needn't handle non-finite values.
Results may differ from a plain program's by a relative error of at most 0.0065.
Values may be sent and summed in bfloat16 or wider, within the bound.
A program may use at most 64 MiB of HBM per device.

v0:
```python
import math


import jax
import jax.numpy as jnp
from jax import lax
from jax.experimental import pallas as pl
from jax.experimental.pallas import tpu as pltpu
from jax.sharding import PartitionSpec as P

H = 64
KVH = 8
DH = 128
LOW = -1e30


def route_by(count, distance):
    return [(i, (i + distance) % count) for i in range(count)]


def pick_kernel(
    table_ref, mig_ref, q_ref, nk_ref, nv_ref, key_ref, value_ref, row_ref, kout_ref, vout_ref, sems
):
    pages = kout_ref.shape[0]
    leaving = mig_ref[lax.axis_index("rep")]

    @pl.loop(0, pages)
    def _(j):
        page = jnp.maximum(table_ref[leaving, j], 0)
        pltpu.make_async_copy(key_ref.at[page], kout_ref.at[j], sems.at[0]).start()
        pltpu.make_async_copy(value_ref.at[page], vout_ref.at[j], sems.at[1]).start()

    at = 0
    for ref in (q_ref, nk_ref, nv_ref):
        width = ref.shape[1]
        slot = lax.broadcasted_iota(jnp.int32, ref.shape, 0)
        chosen = jnp.where(slot == leaving, ref[...].astype(jnp.float32), 0.0)
        row = jnp.sum(chosen, axis=0, keepdims=True)
        row_ref[:, at : at + width] = row.astype(jnp.bfloat16)
        at += width
    pltpu.make_async_copy(key_ref.at[pl.ds(0, pages)], kout_ref, sems.at[0]).wait()
    pltpu.make_async_copy(value_ref.at[pl.ds(0, pages)], vout_ref, sems.at[1]).wait()

    @pl.loop(0, pages)
    def _(j):
        @pl.when(table_ref[leaving, j] < 0)
        def _():
            kout_ref[j] = jnp.zeros(kout_ref.shape[1:], kout_ref.dtype)
            vout_ref[j] = jnp.zeros(vout_ref.shape[1:], vout_ref.dtype)


def picked(table, mig_slot, queries, new_keys, new_values, key_pool, value_pool):
    shape = (table.shape[1],) + key_pool.shape[1:]
    width = queries.shape[1] + 2 * new_keys.shape[1]
    return pl.pallas_call(
        pick_kernel,
        out_shape=[
            jax.ShapeDtypeStruct((1, width), jnp.bfloat16),
            jax.ShapeDtypeStruct(shape, key_pool.dtype),
            jax.ShapeDtypeStruct(shape, key_pool.dtype),
        ],
        in_specs=[pl.BlockSpec(memory_space=pltpu.SMEM)] * 2
        + [pl.BlockSpec(memory_space=pltpu.VMEM)] * 3
        + [pl.BlockSpec(memory_space=pl.ANY)] * 2,
        out_specs=[pl.BlockSpec(memory_space=pltpu.VMEM)] * 3,
        scratch_shapes=[pltpu.SemaphoreType.DMA((2,))],
        compiler_params=pltpu.CompilerParams(vmem_limit_bytes=8 << 20),
        cost_estimate=pl.CostEstimate(
            flops=0, bytes_accessed=8 * math.prod(shape), transcendentals=0
        ),
    )(table, mig_slot, queries, new_keys, new_values, key_pool, value_pool)


def greet(parts):
    me = lax.axis_index("tp")
    barrier = pltpu.get_barrier_semaphore()
    for k in range(1, parts):
        pl.semaphore_signal(
            barrier,
            inc=1,
            device_id={"tp": lax.rem(me + k, parts)},
            device_id_type=pl.DeviceIdType.MESH,
        )
    pl.semaphore_wait(barrier, parts - 1)
    return me


def share_kernel(mig_ref, back_ref, tokens_ref, all_ref, mine_ref, own, send_sems, recv_sems):
    parts, slots, heads_here, _ = all_ref.shape
    chunks = tokens_ref.shape[1]
    leaving = mig_ref[lax.axis_index("rep")]
    back = back_ref[...].astype(jnp.float32)
    row = jnp.concatenate([back[:, h * DH : (h + 1) * DH] for h in range(chunks)], axis=0)
    for i in range(slots):
        value = jnp.where(leaving == i, row, tokens_ref[i].astype(jnp.float32))
        value = value.astype(jnp.bfloat16)
        mine_ref[i] = value
        own[i] = value[:heads_here]
    me = greet(parts)
    copies = []
    for k in range(1, parts):
        copy = pltpu.make_async_remote_copy(
            src_ref=own,
            dst_ref=all_ref.at[me],
            send_sem=send_sems.at[k - 1],
            recv_sem=recv_sems.at[k - 1],
            device_id={"tp": lax.rem(me + k, parts)},
            device_id_type=pl.DeviceIdType.MESH,
        )
        copy.start()
        copies.append(copy)
    all_ref[me] = own[...]
    for copy in copies:
        copy.wait()


def shared(mig_slot, back, tokens, heads_here, parts):
    slots = tokens.shape[0]
    return pl.pallas_call(
        share_kernel,
        out_shape=[
            jax.ShapeDtypeStruct((parts, slots, heads_here, DH), jnp.bfloat16),
            jax.ShapeDtypeStruct(tokens.shape, jnp.bfloat16),
        ],
        in_specs=[pl.BlockSpec(memory_space=pltpu.SMEM)]
        + [pl.BlockSpec(memory_space=pltpu.VMEM)] * 2,
        out_specs=[pl.BlockSpec(memory_space=pltpu.VMEM)] * 2,
        scratch_shapes=[
            pltpu.VMEM((slots, heads_here, DH), jnp.bfloat16),
            pltpu.SemaphoreType.DMA((parts - 1,)),
            pltpu.SemaphoreType.DMA((parts - 1,)),
        ],
        compiler_params=pltpu.CompilerParams(
            collective_id=0, has_side_effects=True, vmem_limit_bytes=8 << 20
        ),
        cost_estimate=pl.CostEstimate(flops=0, bytes_accessed=8 << 20, transcendentals=0),
    )(mig_slot, back, tokens)


def flat_rows(block):
    pages, rows, width = block.shape
    if rows % 16 == 0:
        return block.reshape(pages * rows, width)
    return block.astype(jnp.float32).reshape(pages * rows, width).astype(block.dtype)


def attend_kernel(
    table_ref,
    len_ref,
    start_ref,
    q_ref,
    key_ref,
    value_ref,
    out_ref,
    kbuf,
    vbuf,
    stats_ref,
    ksem,
    vsem,
):
    slots, pages, rows, width = kbuf.shape
    parts, heads_here = q_ref.shape[0], q_ref.shape[2]
    group = H // KVH
    page_len = rows * parts
    scaling = 1.0 / math.sqrt(DH)
    steps = 3 if pages % 3 == 0 else 1
    step_pages = pages // steps

    def live_pages(i):
        return lax.div(len_ref[i] + (page_len - 1), page_len)

    def key_copy(i, j):
        page = jnp.maximum(table_ref[i, j], 0)
        return pltpu.make_async_copy(key_ref.at[page], kbuf.at[i, j], ksem.at[i, j])

    def value_copy(i, j):
        page = jnp.maximum(table_ref[i, j], 0)
        return pltpu.make_async_copy(value_ref.at[page], vbuf.at[i, j], vsem.at[i, j])

    @pl.loop(0, slots)
    def _(i):
        @pl.loop(0, live_pages(i))
        def _(j):
            key_copy(i, j).start()
            value_copy(i, j).start()

    head = lax.broadcasted_iota(jnp.int32, (H, DH), 0) // group
    column = lax.broadcasted_iota(jnp.int32, (H, DH), 1)
    stats_ref[...] = jnp.zeros_like(stats_ref)

    def attend(i, used):
        tokens = used * rows
        lane = lax.broadcasted_iota(jnp.int32, (H, tokens), 1)
        position = (lane // rows) * page_len + lane % rows + start_ref[0]
        q = jnp.concatenate([q_ref[t, i].astype(jnp.float32) for t in range(parts)], axis=0)
        spread = jnp.concatenate(
            [jnp.where(head == g, q, 0.0).astype(jnp.bfloat16) for g in range(KVH)], axis=1
        )
        scores = lax.dot_general(
            spread,
            flat_rows(kbuf[i, 0:used]),
            (((1,), (1,)), ((), ())),
            preferred_element_type=jnp.float32,
        )
        usable = position < len_ref[i]
        masked = jnp.where(usable, scores * scaling, LOW)
        peak = jnp.max(masked, axis=1, keepdims=True)
        weights = jnp.where(usable, jnp.exp(masked - peak), 0.0)
        total = jnp.sum(weights, axis=1, keepdims=True)
        mixed = jnp.dot(
            weights.astype(jnp.bfloat16),
            flat_rows(vbuf[i, 0:used]),
            preferred_element_type=jnp.float32,
        )
        own = jnp.concatenate(
            [
                mixed[g * group : (g + 1) * group, g * DH : (g + 1) * DH]
                for g in range(KVH)
            ],
            axis=0,
        )
        for t in range(parts):
            out_ref[t, i] = own[t * heads_here : (t + 1) * heads_here]
        stats = jnp.where(column == i, peak, stats_ref[...])
        stats_ref[...] = jnp.where(column == i + slots, total, stats)

    @pl.loop(0, slots)
    def _(i):
        live = live_pages(i)
        needed = lax.div(live + (step_pages - 1), step_pages)

        @pl.loop(live, needed * step_pages)
        def _(j):
            vbuf[i, j] = jnp.zeros((rows, width), vbuf.dtype)

        @pl.loop(0, live)
        def _(j):
            key_copy(i, j).wait()
            value_copy(i, j).wait()

        for step in range(1, steps + 1):

            @pl.when(needed == step)
            def _():
                attend(i, step * step_pages)

    for t in range(parts):
        out_ref[t, slots] = stats_ref[t * heads_here : (t + 1) * heads_here]


def attended_parts(table, lens, start, q, key_pool, value_pool, parts):
    slots, pages = table.shape
    rows, width = key_pool.shape[1:]
    buffer = (slots, pages, rows, width)
    return pl.pallas_call(
        attend_kernel,
        out_shape=jax.ShapeDtypeStruct((parts, slots + 1, H // parts, DH), jnp.float32),
        in_specs=[pl.BlockSpec(memory_space=pltpu.SMEM)] * 3
        + [pl.BlockSpec(memory_space=pltpu.VMEM)]
        + [pl.BlockSpec(memory_space=pl.ANY)] * 2,
        out_specs=pl.BlockSpec(memory_space=pltpu.VMEM),
        scratch_shapes=[
            pltpu.VMEM(buffer, key_pool.dtype),
            pltpu.VMEM(buffer, value_pool.dtype),
            pltpu.VMEM((H, DH), jnp.float32),
            pltpu.SemaphoreType.DMA((slots, pages)),
            pltpu.SemaphoreType.DMA((slots, pages)),
        ],
        compiler_params=pltpu.CompilerParams(vmem_limit_bytes=24 << 20),
        cost_estimate=pl.CostEstimate(
            flops=4 * H * pages * rows * width * slots,
            bytes_accessed=4 * math.prod(buffer),
            transcendentals=0,
        ),
    )(table, lens, start, q, key_pool, value_pool)


def finish_kernel(
    mig_ref,
    part_ref,
    mine_ref,
    tk_ref,
    tv_ref,
    out_ref,
    leaver_ref,
    flat,
    landed,
    send_sems,
    recv_sems,
):
    parts, _, heads_here, _ = part_ref.shape
    slots = mine_ref.shape[0]
    repeat = heads_here // tk_ref.shape[1]
    leaving = mig_ref[lax.axis_index("rep")]
    scaling = 1.0 / math.sqrt(DH)
    me = greet(parts)
    copies = []
    for k in range(1, parts):
        peer = lax.rem(me + k, parts)
        copy = pltpu.make_async_remote_copy(
            src_ref=part_ref.at[peer],
            dst_ref=landed.at[k - 1],
            send_sem=send_sems.at[k - 1],
            recv_sem=recv_sems.at[k - 1],
            device_id={"tp": peer},
            device_id_type=pl.DeviceIdType.MESH,
        )
        copy.start()
        copies.append(copy)

    def spread(ref, i):
        value = ref[i].astype(jnp.float32)
        return jnp.concatenate(
            [
                jnp.broadcast_to(value[g : g + 1], (repeat, DH))
                for g in range(value.shape[0])
            ],
            axis=0,
        )

    fresh, values = [], []
    for i in range(slots):
        q = mine_ref[i].astype(jnp.float32)[:heads_here]
        fresh.append(jnp.sum(q * spread(tk_ref, i), axis=-1, keepdims=True) * scaling)
        values.append(spread(tv_ref, i))
    for copy in copies:
        copy.wait()
    stats = [part_ref[me, slots]] + [landed[k, slots] for k in range(parts - 1)]
    leaver = jnp.zeros((heads_here, DH), jnp.float32)
    for i in range(slots):
        top = fresh[i]
        for stat in stats:
            top = jnp.maximum(top, stat[:, i : i + 1])
        weight = jnp.exp(fresh[i] - top)
        total = weight
        mixed = weight.astype(jnp.bfloat16).astype(jnp.float32) * values[i]
        for k, stat in enumerate(stats):
            scale = jnp.exp(stat[:, i : i + 1] - top)
            block = part_ref[me, i] if k == 0 else landed[k - 1, i]
            total = total + scale * stat[:, slots + i : slots + i + 1]
            mixed = mixed + scale * block
        result = mixed / total
        leaver = jnp.where(leaving == i, result, leaver)
        for h in range(heads_here):
            flat[i : i + 1, h * DH : (h + 1) * DH] = result[h : h + 1]
    out_ref[...] = flat[...].astype(out_ref.dtype)
    row = jnp.concatenate([leaver[h : h + 1] for h in range(heads_here)], axis=1)
    leaver_ref[...] = row.astype(leaver_ref.dtype)


def finished(mig_slot, partials, mine, token_keys, token_values):
    parts, _, heads_here, _ = partials.shape
    slots = mine.shape[0]
    return pl.pallas_call(
        finish_kernel,
        out_shape=[
            jax.ShapeDtypeStruct((slots, heads_here * DH), jnp.bfloat16),
            jax.ShapeDtypeStruct((1, heads_here * DH), jnp.bfloat16),
        ],
        in_specs=[pl.BlockSpec(memory_space=pltpu.SMEM)]
        + [pl.BlockSpec(memory_space=pltpu.VMEM)] * 4,
        out_specs=[pl.BlockSpec(memory_space=pltpu.VMEM)] * 2,
        scratch_shapes=[
            pltpu.VMEM((slots, heads_here * DH), jnp.float32),
            pltpu.VMEM((parts - 1,) + partials.shape[1:], jnp.float32),
            pltpu.SemaphoreType.DMA((parts - 1,)),
            pltpu.SemaphoreType.DMA((parts - 1,)),
        ],
        compiler_params=pltpu.CompilerParams(
            collective_id=1, has_side_effects=True, vmem_limit_bytes=8 << 20
        ),
        cost_estimate=pl.CostEstimate(flops=0, bytes_accessed=8 << 20, transcendentals=0),
    )(mig_slot, partials, mine, token_keys, token_values)


def place_kernel(
    mig_ref, result_ref, row_ref, key_ref, value_ref, out_ref, kout_ref, vout_ref, kbuf, vbuf, sems
):
    pages = kbuf.shape[0]
    lanes = ((key_ref, kbuf, kout_ref), (value_ref, vbuf, vout_ref))
    span = 3 if pages % 3 == 0 else 1
    cuts = [pl.ds(j, span) for j in range(0, pages, span)]
    pairs = [(n, c) for c in range(len(cuts)) for n in range(2)]
    for n, c in pairs:
        source, buf, _ = lanes[n]
        pltpu.make_async_copy(source.at[cuts[c]], buf.at[cuts[c]], sems.at[n, c]).start()
    leaving = mig_ref[lax.axis_index("rep")]
    slot = lax.broadcasted_iota(jnp.int32, result_ref.shape, 0)
    row = row_ref[...].astype(jnp.float32)
    result = result_ref[...].astype(jnp.float32)
    out_ref[...] = jnp.where(slot == leaving, row, result).astype(out_ref.dtype)
    for n, c in pairs:
        source, buf, sink = lanes[n]
        pltpu.make_async_copy(source.at[cuts[c]], buf.at[cuts[c]], sems.at[n, c]).wait()
        pltpu.make_async_copy(buf.at[cuts[c]], sink.at[cuts[c]], sems.at[n, c]).start()
    for n, c in pairs:
        _, buf, sink = lanes[n]
        pltpu.make_async_copy(buf.at[cuts[c]], sink.at[cuts[c]], sems.at[n, c]).wait()


def placed_results(mig_slot, result, row, moved_keys, moved_values):
    moved = jax.ShapeDtypeStruct(moved_keys.shape, moved_keys.dtype)
    return pl.pallas_call(
        place_kernel,
        out_shape=[jax.ShapeDtypeStruct(result.shape, result.dtype), moved, moved],
        in_specs=[pl.BlockSpec(memory_space=pltpu.SMEM)]
        + [pl.BlockSpec(memory_space=pltpu.VMEM)] * 2
        + [pl.BlockSpec(memory_space=pl.ANY)] * 2,
        out_specs=[pl.BlockSpec(memory_space=pltpu.VMEM)]
        + [pl.BlockSpec(memory_space=pl.ANY)] * 2,
        scratch_shapes=[
            pltpu.VMEM(moved.shape, moved.dtype),
            pltpu.VMEM(moved.shape, moved.dtype),
            pltpu.SemaphoreType.DMA((2, moved.shape[0])),
        ],
        compiler_params=pltpu.CompilerParams(vmem_limit_bytes=8 << 20),
    )(mig_slot, result, row, moved_keys, moved_values)


def token_rows(fresh, parts, part_index):
    slots, width = fresh.shape
    heads_here = H // parts
    if width % DH == 0:
        return fresh.reshape(slots, width // DH, DH)
    every = lax.all_gather(fresh, "tp", axis=1, tiled=True).reshape(slots, KVH, DH)
    every = jnp.repeat(every, H // KVH, axis=1)
    return lax.dynamic_slice_in_dim(every, part_index * heads_here, heads_here, 1)


def body(
    queries, new_keys, new_values, key_pool, value_pool, lengths, page_table, mig_slot, mig_dst
):
    replicas = lax.axis_size("rep")
    parts = lax.axis_size("tp")
    here_rep = lax.axis_index("rep")
    part_index = lax.axis_index("tp")
    slots, _ = queries.shape
    k_width = new_keys.shape[1]
    heads_here = H // parts
    offset = mig_dst[0]
    start = (part_index * key_pool.shape[1]).reshape(1)
    visitor, keys_out, values_out = picked(
        page_table, mig_slot, queries, new_keys, new_values, key_pool, value_pool
    )

    def branch(distance):
        def run(visitor, keys_out, values_out):
            back = lax.ppermute(visitor, "rep", route_by(replicas, -distance))
            moved_keys = lax.ppermute(keys_out, "rep", route_by(replicas, distance))
            moved_values = lax.ppermute(values_out, "rep", route_by(replicas, distance))
            own_len = lax.dynamic_slice_in_dim(lengths, here_rep * slots, slots)
            tokens = jnp.concatenate([queries, new_keys, new_values], axis=1)
            tokens = tokens.reshape(slots, -1, DH)
            q_all, mine = shared(mig_slot, back, tokens, heads_here, parts)
            flat = mine[:, heads_here:].reshape(slots, 2 * k_width)
            token_keys = token_rows(flat[:, :k_width], parts, part_index)
            token_values = token_rows(flat[:, k_width:], parts, part_index)
            partials = attended_parts(
                page_table, own_len, start, q_all, key_pool, value_pool, parts
            )
            result, leaver = finished(mig_slot, partials, mine, token_keys, token_values)
            arrived = lax.ppermute(leaver, "rep", route_by(replicas, distance))
            return result, arrived, moved_keys, moved_values

        return run

    result, arrived, moved_keys, moved_values = lax.switch(
        offset - 1,
        [branch(distance) for distance in range(1, replicas)],
        visitor,
        keys_out,
        values_out,
    )
    return placed_results(mig_slot, result, arrived, moved_keys, moved_values)


def solution(mesh):
    placed = (
        P("rep", "tp"),
        P("rep", "tp"),
        P("rep", "tp"),
        P("rep", "tp", None),
        P("rep", "tp", None),
        P(),
        P("rep", None),
        P(),
        P(),
    )
    return jax.shard_map(
        body,
        mesh=mesh,
        in_specs=placed,
        out_specs=(P("rep", "tp"), P("rep", "tp", None), P("rep", "tp", None)),
        check_vma=False,
    )
```

profile of v0, /device:TPU:0, one launch (start us, length us, event | category | flops | bytes accessed | tf_op | source)
XLA Modules:
  0.0 74.3 jit_solution(3639094761545985599)
XLA Ops:
  1.3 0.0 copy-start
  1.3 0.0 copy-start.1
  1.3 0.0 copy-start.2
  1.3 0.0 copy-start.3
  1.3 0.0 copy-start.4
  1.3 0.0 copy-start.5
  1.3 2.4 %shard_map.112 = (bf16[1,2560]{1,0:T(2,128)(2,1)S(1)}, bf16[12,32,1024]{2,1,0:T(8,128)(2,1)S(1)}, bf16[12,32,1024]{2,1,0:T(8,128)(2,1)S(1)}) custom-call(s32[8,12]{1,0:T(8,128)} %table_ref.1, s32[8]{0:T(128)} %mig_ref.3, bf16[8,2048]{1,0:T(8,128)(2,1)} %q_ref.1, bf16[8,256]{1,0:T(8,128)(2,1)} %nk_ref.1, bf16[8,256]{1,0:T(8,128)(2,1)} %nv_ref.1, ...), custom_call_target="tpu_custom_call" | custom-call | bytes 3145728 | tf_op jit(solution)/shard_map/pallas_call | solution.py:55
  3.8 0.0 copy-done
  3.8 0.0 copy-done.1
  3.8 0.0 copy-done.2
  3.8 0.0 copy-done.3
  3.8 0.0 copy-done.4
  3.8 0.0 copy-done.5
  3.8 66.7 %conditional.1 = (bf16[8,2048]{1,0:T(8,128)(2,1)S(1)}, bf16[1,2048]{1,0:T(2,128)(2,1)}, bf16[12,32,1024]{2,1,0:T(8,128)(2,1)}, bf16[12,32,1024]{2,1,0:T(8,128)(2,1)}) conditional(s32[]{:T(128)} %bitcast.7, (s32[]{:T(128)}, s32[64]{0:T(128)S(1)}, bf16[1,2560]{1,0:T(2,128)(2,1)S(1)}, bf16[8,2048]{1,0:T(8,128)(2,1)S(1)}, ...), branch_computations={%region_0.0_spmd, %region_1.0_spmd, %region_2.0_spmd, %region_3.0_... | conditional | flops 805429248 | bytes 35918128 | solution.py:467
  3.9 6.0 %collective-permute-start.22 = (bf16[12,32,1024]{2,1,0:T(8,128)(2,1)S(1)}, bf16[12,32,1024]{2,1,0:T(8,128)(2,1)}, u32[]{:S(2)}, u32[]{:S(2)}) collective-permute-start(bf16[12,32,1024]{2,1,0:T(8,128)(2,1)S(1)} %get-tuple-element.282), channel_id=1, source_target_pairs={{0,24},{4,28},{8,0},{12,4},{16,8},{20,12},{24,16},{28,20},{1,25},{... | collective-permute-start | bytes 2359304 | tf_op jit(solution)/shard_map/cond/branch_5_fun/ppermute | solution.py:449
  9.9 0.2 collective-permute-start.23
  10.1 1.9 %collective-permute-start.20 = (bf16[1,2560]{1,0:T(2,128)(2,1)S(1)}, bf16[1,2560]{1,0:T(2,128)(2,1)S(1)}, u32[]{:S(2)}, u32[]{:S(2)}) collective-permute-start(bf16[1,2560]{1,0:T(2,128)(2,1)S(1)} %get-tuple-element.272), channel_id=1, source_target_pairs={{0,8},{4,12},{8,16},{12,20},{16,24},{20,28},{24,0},{28,4},{1,9},{5... | collective-permute-start | bytes 15368 | tf_op jit(solution)/shard_map/cond/branch_5_fun/ppermute | solution.py:448
  12.0 0.1 dynamic_slice.19.len_ref
  12.0 31.6 %collective-permute-done.20.back_ref = bf16[1,2560]{1,0:T(2,128)(2,1)S(1)} collective-permute-done((bf16[1,2560]{1,0:T(2,128)(2,1)S(1)}, bf16[1,2560]{1,0:T(2,128)(2,1)S(1)}, u32[]{:S(2)}, u32[]{:S(2)}) %collective-permute-start.20) | collective-permute-done | bytes 5152 | tf_op jit(solution)/shard_map/cond/branch_5_fun/ppermute | solution.py:448
  43.7 5.9 %branch_5_fun.3 = (bf16[4,8,16,128]{3,2,1,0:T(8,128)(2,1)S(1)}, bf16[8,20,128]{2,1,0:T(8,128)(2,1)S(1)}) custom-call(s32[8]{0:T(128)S(1)} %get-tuple-element.267.mig_ref, bf16[1,2560]{1,0:T(2,128)(2,1)S(1)} %collective-permute-done.20.back_ref, bf16[8,20,128]{2,1,0:T(8,128)(2,1)S(1)} %copy.17.tokens_ref), custom_call_target="tpu_custom_call" | custom-call | bytes 8388608 | tf_op jit(solution)/shard_map/cond/branch_5_fun/pallas_call | solution.py:119
  49.6 9.6 %branch_5_fun.4.part_ref = f32[4,9,16,128]{3,2,1,0:T(8,128)S(1)} custom-call(s32[8,12]{1,0:T(8,128)S(1)} %get-tuple-element.268.table_ref, s32[8]{0:T(128)S(1)} %dynamic_slice.19.len_ref, s32[1]{0:T(128)} %get-tuple-element.271.start_ref, bf16[4,8,16,128]{3,2,1,0:T(8,128)(2,1)S(1)} %get-tuple-element.276.q_ref, ...), custom_call_target="tpu_custom_call" | custom-call | flops 805306368 | bytes 12582912 | tf_op jit(solution)/shard_map/cond/branch_5_fun/pallas_call | solution.py:255
  59.3 6.9 %branch_5_fun.5 = (bf16[8,2048]{1,0:T(8,128)(2,1)S(1)}, bf16[1,2048]{1,0:T(2,128)(2,1)S(1)}) custom-call(s32[8]{0:T(128)S(1)} %get-tuple-element.267.mig_ref, f32[4,9,16,128]{3,2,1,0:T(8,128)S(1)} %branch_5_fun.4.part_ref, bf16[8,20,128]{2,1,0:T(8,128)(2,1)S(1)} %get-tuple-element.279.mine_ref, bf16[8,2,128]{2,1,0:T(2,128)(2,1)S(1)} %reshape.91.tk_ref, ...), custom_call_target="tpu_custom_call" | custom-call | bytes 8388608 | tf_op jit(solution)/shard_map/cond/branch_5_fun/pallas_call | solution.py:354
  66.2 3.0 %collective-permute-start.21 = (bf16[1,2048]{1,0:T(2,128)(2,1)S(1)}, bf16[1,2048]{1,0:T(2,128)(2,1)}, u32[]{:S(2)}, u32[]{:S(2)}) collective-permute-start(bf16[1,2048]{1,0:T(2,128)(2,1)S(1)} %get-tuple-element.281), channel_id=1, source_target_pairs={{0,24},{4,28},{8,0},{12,4},{16,8},{20,12},{24,16},{28,20},{1,25},{... | collective-permute-start | bytes 12296 | tf_op jit(solution)/shard_map/cond/branch_5_fun/ppermute | solution.py:462
  69.2 1.4 %collective-permute-done.21 = bf16[1,2048]{1,0:T(2,128)(2,1)} collective-permute-done((bf16[1,2048]{1,0:T(2,128)(2,1)S(1)}, bf16[1,2048]{1,0:T(2,128)(2,1)}, u32[]{:S(2)}, u32[]{:S(2)}) %collective-permute-start.21) | collective-permute-done | bytes 4128 | tf_op jit(solution)/shard_map/cond/branch_5_fun/ppermute | solution.py:462
  70.6 0.0 collective-permute-done.22
  70.6 0.0 collective-permute-done.23
  70.6 3.7 %shard_map.113 = (bf16[8,2048]{1,0:T(8,128)(2,1)}, bf16[12,32,1024]{2,1,0:T(8,128)(2,1)}, bf16[12,32,1024]{2,1,0:T(8,128)(2,1)}) custom-call(s32[8]{0:T(128)S(1)} %copy-done.4, bf16[8,2048]{1,0:T(8,128)(2,1)S(1)} %get-tuple-element.314.result_ref, bf16[1,2048]{1,0:T(2,128)(2,1)} %get-tuple-element.315.row_ref, ...), custom_call_target="tpu_custom_call" | custom-call | tf_op jit(solution)/shard_map/pallas_call | solution.py:403
  (7 shorter events, 0.1 us)
Async XLA Ops:
  1.3 2.5 %copy-start = (bf16[8,2048]{1,0:T(8,128)(2,1)S(1)}, bf16[8,2048]{1,0:T(8,128)(2,1)}, u32[]{:S(2)}) copy-start(bf16[8,2048]{1,0:T(8,128)(2,1)} %q_ref.1) | copy-start | bytes 98308
  1.3 2.5 %copy-start.1 = (s32[8,12]{1,0:T(8,128)S(1)}, s32[8,12]{1,0:T(8,128)}, u32[]{:S(2)}) copy-start(s32[8,12]{1,0:T(8,128)} %table_ref.1) | copy-start | bytes 1156
  1.3 2.5 %copy-start.2 = (bf16[8,256]{1,0:T(8,128)(2,1)S(1)}, bf16[8,256]{1,0:T(8,128)(2,1)}, u32[]{:S(2)}) copy-start(bf16[8,256]{1,0:T(8,128)(2,1)} %nk_ref.1) | copy-start | bytes 12292
  1.3 2.5 %copy-start.3 = (bf16[8,256]{1,0:T(8,128)(2,1)S(1)}, bf16[8,256]{1,0:T(8,128)(2,1)}, u32[]{:S(2)}) copy-start(bf16[8,256]{1,0:T(8,128)(2,1)} %nv_ref.1) | copy-start | bytes 12292
  1.3 2.5 %copy-start.4 = (s32[8]{0:T(128)S(1)}, s32[8]{0:T(128)}, u32[]{:S(2)}) copy-start(s32[8]{0:T(128)} %mig_ref.3) | copy-start | bytes 100
  1.3 2.5 %copy-start.5 = (s32[64]{0:T(128)S(1)}, s32[64]{0:T(128)}, u32[]{:S(2)}) copy-start(s32[64]{0:T(128)} %param.21) | copy-start | bytes 772
  3.9 66.7 %collective-permute-start.22 = (bf16[12,32,1024]{2,1,0:T(8,128)(2,1)S(1)}, bf16[12,32,1024]{2,1,0:T(8,128)(2,1)}, u32[]{:S(2)}, u32[]{:S(2)}) collective-permute-start(bf16[12,32,1024]{2,1,0:T(8,128)(2,1)S(1)} %get-tuple-element.282), channel_id=1, source_target_pairs={{0,24},{4,28},{8,0},{12,4},{16,8},{20,12},{24,16},{28,20},{1,25},{... | collective-permute-start | bytes 2359304 | tf_op jit(solution)/shard_map/cond/branch_5_fun/ppermute | solution.py:449
  9.9 60.7 %collective-permute-start.23 = (bf16[12,32,1024]{2,1,0:T(8,128)(2,1)S(1)}, bf16[12,32,1024]{2,1,0:T(8,128)(2,1)}, u32[]{:S(2)}, u32[]{:S(2)}) collective-permute-start(bf16[12,32,1024]{2,1,0:T(8,128)(2,1)S(1)} %get-tuple-element.283), channel_id=1, source_target_pairs={{0,24},{4,28},{8,0},{12,4},{16,8},{20,12},{24,16},{28,20},{1,25},{... | collective-permute-start | bytes 2359304 | tf_op jit(solution)/shard_map/cond/branch_5_fun/ppermute | solution.py:450
  10.1 33.6 %collective-permute-start.20 = (bf16[1,2560]{1,0:T(2,128)(2,1)S(1)}, bf16[1,2560]{1,0:T(2,128)(2,1)S(1)}, u32[]{:S(2)}, u32[]{:S(2)}) collective-permute-start(bf16[1,2560]{1,0:T(2,128)(2,1)S(1)} %get-tuple-element.272), channel_id=1, source_target_pairs={{0,8},{4,12},{8,16},{12,20},{16,24},{20,28},{24,0},{28,4},{1,9},{5... | collective-permute-start | bytes 15368 | tf_op jit(solution)/shard_map/cond/branch_5_fun/ppermute | solution.py:448
  66.2 4.4 %collective-permute-start.21 = (bf16[1,2048]{1,0:T(2,128)(2,1)S(1)}, bf16[1,2048]{1,0:T(2,128)(2,1)}, u32[]{:S(2)}, u32[]{:S(2)}) collective-permute-start(bf16[1,2048]{1,0:T(2,128)(2,1)S(1)} %get-tuple-element.281), channel_id=1, source_target_pairs={{0,24},{4,28},{8,0},{12,4},{16,8},{20,12},{24,16},{28,20},{1,25},{... | collective-permute-start | bytes 12296 | tf_op jit(solution)/shard_map/cond/branch_5_fun/ppermute | solution.py:462
where the time goes:
time: 74.6 us; the launch traced here: 74.3 us
  waiting for transfers between devices  33 us (44%)
  Pallas kernels  28.5 us (38%)
  starting transfers between devices  11.1 us (15%)
  between operations  1.39 us (2%)
    ppermute x1, waiting for transfers between devices, run(): back = lax.ppermute(visitor, 'rep', route_by(replicas, -distance))  31.6 us
    pallas_call x1, Pallas kernels, attended_parts(): pl.pallas_call(attend_kernel, out_shape=jax.ShapeDtypeStruct((parts, slot...  9.62 us
    pallas_call x1, Pallas kernels, finished(): pl.pallas_call(finish_kernel, out_shape=[jax.ShapeDtypeStruct((slots, hea...  6.9 us
    ppermute x1, starting transfers between devices, run(): moved_keys = lax.ppermute(keys_out, 'rep', route_by(replicas, distance))  6.03 us
    pallas_call x1, Pallas kernels, shared(): pl.pallas_call(share_kernel, out_shape=[jax.ShapeDtypeStruct((parts, slot...  5.88 us
    pallas_call x1, Pallas kernels, placed_results(): pl.pallas_call(place_kernel, out_shape=[jax.ShapeDtypeStruct(result.shape...  3.68 us
    ppermute x1, starting transfers between devices, run(): arrived = lax.ppermute(leaver, 'rep', route_by(replicas, distance))  3.03 us
    pallas_call x1, Pallas kernels, picked(): pl.pallas_call(pick_kernel, out_shape=[jax.ShapeDtypeStruct((1, width), j...  2.43 us
  transfers between devices with their start and end apart: 4, of which 2 were waited for; matrix products, arithmetic and copies ran while one was open for 0% of the time, Pallas kernels for 30%

commit v1 on v0

--- a/solution.py
+++ b/solution.py
@@ -19,8 +19,25 @@
 
 
 def pick_kernel(
-    table_ref, mig_ref, q_ref, nk_ref, nv_ref, key_ref, value_ref, row_ref, kout_ref, vout_ref, sems
+    table_ref,
+    mig_ref,
+    q_ref,
+    nk_ref,
+    nv_ref,
+    key_ref,
+    value_ref,
+    row_ref,
+    kout_ref,
+    vout_ref,
+    q_buf,
+    nk_buf,
+    nv_buf,
+    sems,
+    row_sems,
 ):
+    fills = ((q_ref, q_buf), (nk_ref, nk_buf), (nv_ref, nv_buf))
+    for n, (ref, buf) in enumerate(fills):
+        pltpu.make_async_copy(ref, buf, row_sems.at[n]).start()
     pages = kout_ref.shape[0]
     leaving = mig_ref[lax.axis_index("rep")]
 
@@ -31,10 +48,11 @@
         pltpu.make_async_copy(value_ref.at[page], vout_ref.at[j], sems.at[1]).start()
 
     at = 0
-    for ref in (q_ref, nk_ref, nv_ref):
-        width = ref.shape[1]
-        slot = lax.broadcasted_iota(jnp.int32, ref.shape, 0)
-        chosen = jnp.where(slot == leaving, ref[...].astype(jnp.float32), 0.0)
+    for n, (ref, buf) in enumerate(fills):
+        pltpu.make_async_copy(ref, buf, row_sems.at[n]).wait()
+        width = buf.shape[1]
+        slot = lax.broadcasted_iota(jnp.int32, buf.shape, 0)
+        chosen = jnp.where(slot == leaving, buf[...].astype(jnp.float32), 0.0)
         row = jnp.sum(chosen, axis=0, keepdims=True)
         row_ref[:, at : at + width] = row.astype(jnp.bfloat16)
         at += width
@@ -60,10 +78,15 @@
             jax.ShapeDtypeStruct(shape, key_pool.dtype),
         ],
         in_specs=[pl.BlockSpec(memory_space=pltpu.SMEM)] * 2
-        + [pl.BlockSpec(memory_space=pltpu.VMEM)] * 3
-        + [pl.BlockSpec(memory_space=pl.ANY)] * 2,
+        + [pl.BlockSpec(memory_space=pl.ANY)] * 5,
         out_specs=[pl.BlockSpec(memory_space=pltpu.VMEM)] * 3,
-        scratch_shapes=[pltpu.SemaphoreType.DMA((2,))],
+        scratch_shapes=[
+            pltpu.VMEM(queries.shape, queries.dtype),
+            pltpu.VMEM(new_keys.shape, new_keys.dtype),
+            pltpu.VMEM(new_values.shape, new_values.dtype),
+            pltpu.SemaphoreType.DMA((2,)),
+            pltpu.SemaphoreType.DMA((3,)),
+        ],
         compiler_params=pltpu.CompilerParams(vmem_limit_bytes=8 << 20),
         cost_estimate=pl.CostEstimate(
             flops=0, bytes_accessed=8 * math.prod(shape), transcendentals=0
@@ -374,9 +397,24 @@
 
 
 def place_kernel(
-    mig_ref, result_ref, row_ref, key_ref, value_ref, out_ref, kout_ref, vout_ref, kbuf, vbuf, sems
+    mig_ref,
+    result_ref,
+    row_ref,
+    key_ref,
+    value_ref,
+    out_ref,
+    kout_ref,
+    vout_ref,
+    kbuf,
+    vbuf,
+    rowbuf,
+    outbuf,
+    sems,
+    row_sem,
+    out_sem,
 ):
     pages = kbuf.shape[0]
+    pltpu.make_async_copy(row_ref, rowbuf, row_sem).start()
     lanes = ((key_ref, kbuf, kout_ref), (value_ref, vbuf, vout_ref))
     span = 3 if pages % 3 == 0 else 1
     cuts = [pl.ds(j, span) for j in range(0, pages, span)]
@@ -386,16 +424,19 @@
         pltpu.make_async_copy(source.at[cuts[c]], buf.at[cuts[c]], sems.at[n, c]).start()
     leaving = mig_ref[lax.axis_index("rep")]
     slot = lax.broadcasted_iota(jnp.int32, result_ref.shape, 0)
-    row = row_ref[...].astype(jnp.float32)
+    pltpu.make_async_copy(row_ref, rowbuf, row_sem).wait()
+    row = rowbuf[...].astype(jnp.float32)
     result = result_ref[...].astype(jnp.float32)
-    out_ref[...] = jnp.where(slot == leaving, row, result).astype(out_ref.dtype)
+    outbuf[...] = jnp.where(slot == leaving, row, result).astype(outbuf.dtype)
     for n, c in pairs:
         source, buf, sink = lanes[n]
         pltpu.make_async_copy(source.at[cuts[c]], buf.at[cuts[c]], sems.at[n, c]).wait()
         pltpu.make_async_copy(buf.at[cuts[c]], sink.at[cuts[c]], sems.at[n, c]).start()
+    pltpu.make_async_copy(outbuf, out_ref, out_sem).start()
     for n, c in pairs:
         _, buf, sink = lanes[n]
         pltpu.make_async_copy(buf.at[cuts[c]], sink.at[cuts[c]], sems.at[n, c]).wait()
+    pltpu.make_async_copy(outbuf, out_ref, out_sem).wait()
 
 
 def placed_results(mig_slot, result, row, moved_keys, moved_values):
@@ -404,14 +445,17 @@
         place_kernel,
         out_shape=[jax.ShapeDtypeStruct(result.shape, result.dtype), moved, moved],
         in_specs=[pl.BlockSpec(memory_space=pltpu.SMEM)]
-        + [pl.BlockSpec(memory_space=pltpu.VMEM)] * 2
-        + [pl.BlockSpec(memory_space=pl.ANY)] * 2,
-        out_specs=[pl.BlockSpec(memory_space=pltpu.VMEM)]
-        + [pl.BlockSpec(memory_space=pl.ANY)] * 2,
+        + [pl.BlockSpec(memory_space=pltpu.VMEM)]
+        + [pl.BlockSpec(memory_space=pl.ANY)] * 3,
+        out_specs=[pl.BlockSpec(memory_space=pl.ANY)] * 3,
         scratch_shapes=[
             pltpu.VMEM(moved.shape, moved.dtype),
             pltpu.VMEM(moved.shape, moved.dtype),
+            pltpu.VMEM(row.shape, row.dtype),
+            pltpu.VMEM(result.shape, result.dtype),
             pltpu.SemaphoreType.DMA((2, moved.shape[0])),
+            pltpu.SemaphoreType.DMA,
+            pltpu.SemaphoreType.DMA,
         ],
         compiler_params=pltpu.CompilerParams(vmem_limit_bytes=8 << 20),
     )(mig_slot, result, row, moved_keys, moved_values)

time: 74.6 us -> 74.1 us (level)
  no operation moved by 1% of the time
where the time goes in v1:
time: 74.1 us; the launch traced here: 73.8 us
  waiting for transfers between devices  33 us (45%)
  Pallas kernels  28 us (38%)
  starting transfers between devices  11.1 us (15%)
  between operations  1.39 us (2%)
    ppermute x1, waiting for transfers between devices, run(): back = lax.ppermute(visitor, 'rep', route_by(replicas, -distance))  31.7 us
    pallas_call x1, Pallas kernels, attended_parts(): pl.pallas_call(attend_kernel, out_shape=jax.ShapeDtypeStruct((parts, slot...  9.62 us
    pallas_call x1, Pallas kernels, finished(): pl.pallas_call(finish_kernel, out_shape=[jax.ShapeDtypeStruct((slots, hea...  6.9 us
    ppermute x1, starting transfers between devices, run(): moved_keys = lax.ppermute(keys_out, 'rep', route_by(replicas, distance))  6.03 us
    pallas_call x1, Pallas kernels, shared(): pl.pallas_call(share_kernel, out_shape=[jax.ShapeDtypeStruct((parts, slot...  5.88 us
    pallas_call x1, Pallas kernels, placed_results(): pl.pallas_call(place_kernel, out_shape=[jax.ShapeDtypeStruct(result.shape...  3.13 us
    ppermute x1, starting transfers between devices, run(): arrived = lax.ppermute(leaver, 'rep', route_by(replicas, distance))  3.03 us
    pallas_call x1, Pallas kernels, picked(): pl.pallas_call(pick_kernel, out_shape=[jax.ShapeDtypeStruct((1, width), j...  2.45 us
  transfers between devices with their start and end apart: 4, of which 2 were waited for; matrix products, arithmetic and copies ran while one was open for 0% of the time, Pallas kernels for 30%

profile of v1, /device:TPU:0, one launch (start us, length us, event | category | flops | bytes accessed | tf_op | source)
XLA Modules:
  0.0 73.8 jit_solution(5249607174319925382)
XLA Ops:
  1.3 0.0 copy-start
  1.3 0.0 copy-start.1
  1.3 0.0 copy-start.2
  1.3 0.0 copy-start.3
  1.3 0.0 copy-start.4
  1.3 0.0 copy-start.5
  1.3 2.5 %shard_map.112 = (bf16[1,2560]{1,0:T(2,128)(2,1)S(1)}, bf16[12,32,1024]{2,1,0:T(8,128)(2,1)S(1)}, bf16[12,32,1024]{2,1,0:T(8,128)(2,1)S(1)}) custom-call(s32[8,12]{1,0:T(8,128)} %table_ref.1, s32[8]{0:T(128)} %mig_ref.3, bf16[8,2048]{1,0:T(8,128)(2,1)} %q_ref.1, bf16[8,256]{1,0:T(8,128)(2,1)} %nk_ref.1, bf16[8,256]{1,0:T(8,128)(2,1)} %nv_ref.1, ...), custom_call_target="tpu_custom_call" | custom-call | bytes 3145728 | tf_op jit(solution)/shard_map/pallas_call | solution.py:73
  3.8 0.0 copy-done
  3.8 0.0 copy-done.1
  3.8 0.0 copy-done.2
  3.8 0.0 copy-done.3
  3.8 0.0 copy-done.4
  3.9 0.0 copy-done.5
  3.9 66.8 %conditional.1 = (bf16[8,2048]{1,0:T(8,128)(2,1)S(1)}, bf16[1,2048]{1,0:T(2,128)(2,1)}, bf16[12,32,1024]{2,1,0:T(8,128)(2,1)}, bf16[12,32,1024]{2,1,0:T(8,128)(2,1)}) conditional(s32[]{:T(128)} %bitcast.7, (s32[]{:T(128)}, s32[64]{0:T(128)S(1)}, bf16[1,2560]{1,0:T(2,128)(2,1)S(1)}, bf16[8,2048]{1,0:T(8,128)(2,1)S(1)}, ...), branch_computations={%region_0.0_spmd, %region_1.0_spmd, %region_2.0_spmd, %region_3.0_... | conditional | flops 805429248 | bytes 35918128 | solution.py:511
  3.9 6.0 %collective-permute-start.22 = (bf16[12,32,1024]{2,1,0:T(8,128)(2,1)S(1)}, bf16[12,32,1024]{2,1,0:T(8,128)(2,1)}, u32[]{:S(2)}, u32[]{:S(2)}) collective-permute-start(bf16[12,32,1024]{2,1,0:T(8,128)(2,1)S(1)} %get-tuple-element.282), channel_id=1, source_target_pairs={{0,24},{4,28},{8,0},{12,4},{16,8},{20,12},{24,16},{28,20},{1,25},{... | collective-permute-start | bytes 2359304 | tf_op jit(solution)/shard_map/cond/branch_5_fun/ppermute | solution.py:493
  9.9 0.2 collective-permute-start.23
  10.1 1.9 %collective-permute-start.20 = (bf16[1,2560]{1,0:T(2,128)(2,1)S(1)}, bf16[1,2560]{1,0:T(2,128)(2,1)S(1)}, u32[]{:S(2)}, u32[]{:S(2)}) collective-permute-start(bf16[1,2560]{1,0:T(2,128)(2,1)S(1)} %get-tuple-element.272), channel_id=1, source_target_pairs={{0,8},{4,12},{8,16},{12,20},{16,24},{20,28},{24,0},{28,4},{1,9},{5... | collective-permute-start | bytes 15368 | tf_op jit(solution)/shard_map/cond/branch_5_fun/ppermute | solution.py:492
  12.0 0.1 dynamic_slice.19.len_ref
  12.1 31.7 %collective-permute-done.20.back_ref = bf16[1,2560]{1,0:T(2,128)(2,1)S(1)} collective-permute-done((bf16[1,2560]{1,0:T(2,128)(2,1)S(1)}, bf16[1,2560]{1,0:T(2,128)(2,1)S(1)}, u32[]{:S(2)}, u32[]{:S(2)}) %collective-permute-start.20) | collective-permute-done | bytes 5152 | tf_op jit(solution)/shard_map/cond/branch_5_fun/ppermute | solution.py:492
  43.7 5.9 %branch_5_fun.3 = (bf16[4,8,16,128]{3,2,1,0:T(8,128)(2,1)S(1)}, bf16[8,20,128]{2,1,0:T(8,128)(2,1)S(1)}) custom-call(s32[8]{0:T(128)S(1)} %get-tuple-element.267.mig_ref, bf16[1,2560]{1,0:T(2,128)(2,1)S(1)} %collective-permute-done.20.back_ref, bf16[8,20,128]{2,1,0:T(8,128)(2,1)S(1)} %copy.17.tokens_ref), custom_call_target="tpu_custom_call" | custom-call | bytes 8388608 | tf_op jit(solution)/shard_map/cond/branch_5_fun/pallas_call | solution.py:142
  49.7 9.6 %branch_5_fun.4.part_ref = f32[4,9,16,128]{3,2,1,0:T(8,128)S(1)} custom-call(s32[8,12]{1,0:T(8,128)S(1)} %get-tuple-element.268.table_ref, s32[8]{0:T(128)S(1)} %dynamic_slice.19.len_ref, s32[1]{0:T(128)} %get-tuple-element.271.start_ref, bf16[4,8,16,128]{3,2,1,0:T(8,128)(2,1)S(1)} %get-tuple-element.276.q_ref, ...), custom_call_target="tpu_custom_call" | custom-call | flops 805306368 | bytes 12582912 | tf_op jit(solution)/shard_map/cond/branch_5_fun/pallas_call | solution.py:278
  59.3 6.9 %branch_5_fun.5 = (bf16[8,2048]{1,0:T(8,128)(2,1)S(1)}, bf16[1,2048]{1,0:T(2,128)(2,1)S(1)}) custom-call(s32[8]{0:T(128)S(1)} %get-tuple-element.267.mig_ref, f32[4,9,16,128]{3,2,1,0:T(8,128)S(1)} %branch_5_fun.4.part_ref, bf16[8,20,128]{2,1,0:T(8,128)(2,1)S(1)} %get-tuple-element.279.mine_ref, bf16[8,2,128]{2,1,0:T(2,128)(2,1)S(1)} %reshape.91.tk_ref, ...), custom_call_target="tpu_custom_call" | custom-call | bytes 8388608 | tf_op jit(solution)/shard_map/cond/branch_5_fun/pallas_call | solution.py:377
  66.2 3.0 %collective-permute-start.21 = (bf16[1,2048]{1,0:T(2,128)(2,1)S(1)}, bf16[1,2048]{1,0:T(2,128)(2,1)}, u32[]{:S(2)}, u32[]{:S(2)}) collective-permute-start(bf16[1,2048]{1,0:T(2,128)(2,1)S(1)} %get-tuple-element.281), channel_id=1, source_target_pairs={{0,24},{4,28},{8,0},{12,4},{16,8},{20,12},{24,16},{28,20},{1,25},{... | collective-permute-start | bytes 12296 | tf_op jit(solution)/shard_map/cond/branch_5_fun/ppermute | solution.py:506
  69.3 1.4 %collective-permute-done.21 = bf16[1,2048]{1,0:T(2,128)(2,1)} collective-permute-done((bf16[1,2048]{1,0:T(2,128)(2,1)S(1)}, bf16[1,2048]{1,0:T(2,128)(2,1)}, u32[]{:S(2)}, u32[]{:S(2)}) %collective-permute-start.21) | collective-permute-done | bytes 4128 | tf_op jit(solution)/shard_map/cond/branch_5_fun/ppermute | solution.py:506
  70.6 0.0 collective-permute-done.22
  70.6 0.0 collective-permute-done.23
  70.6 3.1 %shard_map.113 = (bf16[8,2048]{1,0:T(8,128)(2,1)}, bf16[12,32,1024]{2,1,0:T(8,128)(2,1)}, bf16[12,32,1024]{2,1,0:T(8,128)(2,1)}) custom-call(s32[8]{0:T(128)S(1)} %copy-done.4, bf16[8,2048]{1,0:T(8,128)(2,1)S(1)} %get-tuple-element.314.result_ref, bf16[1,2048]{1,0:T(2,128)(2,1)} %get-tuple-element.315.row_ref, ...), custom_call_target="tpu_custom_call" | custom-call | tf_op jit(solution)/shard_map/pallas_call | solution.py:444
  (7 shorter events, 0.1 us)
Async XLA Ops:
  1.3 2.5 %copy-start = (bf16[8,2048]{1,0:T(8,128)(2,1)S(1)}, bf16[8,2048]{1,0:T(8,128)(2,1)}, u32[]{:S(2)}) copy-start(bf16[8,2048]{1,0:T(8,128)(2,1)} %q_ref.1) | copy-start | bytes 98308
  1.3 2.5 %copy-start.1 = (s32[8,12]{1,0:T(8,128)S(1)}, s32[8,12]{1,0:T(8,128)}, u32[]{:S(2)}) copy-start(s32[8,12]{1,0:T(8,128)} %table_ref.1) | copy-start | bytes 1156
  1.3 2.5 %copy-start.2 = (bf16[8,256]{1,0:T(8,128)(2,1)S(1)}, bf16[8,256]{1,0:T(8,128)(2,1)}, u32[]{:S(2)}) copy-start(bf16[8,256]{1,0:T(8,128)(2,1)} %nk_ref.1) | copy-start | bytes 12292
  1.3 2.5 %copy-start.3 = (bf16[8,256]{1,0:T(8,128)(2,1)S(1)}, bf16[8,256]{1,0:T(8,128)(2,1)}, u32[]{:S(2)}) copy-start(bf16[8,256]{1,0:T(8,128)(2,1)} %nv_ref.1) | copy-start | bytes 12292
  1.3 2.5 %copy-start.4 = (s32[8]{0:T(128)S(1)}, s32[8]{0:T(128)}, u32[]{:S(2)}) copy-start(s32[8]{0:T(128)} %mig_ref.3) | copy-start | bytes 100
  1.3 2.5 %copy-start.5 = (s32[64]{0:T(128)S(1)}, s32[64]{0:T(128)}, u32[]{:S(2)}) copy-start(s32[64]{0:T(128)} %param.21) | copy-start | bytes 772
  3.9 66.7 %collective-permute-start.22 = (bf16[12,32,1024]{2,1,0:T(8,128)(2,1)S(1)}, bf16[12,32,1024]{2,1,0:T(8,128)(2,1)}, u32[]{:S(2)}, u32[]{:S(2)}) collective-permute-start(bf16[12,32,1024]{2,1,0:T(8,128)(2,1)S(1)} %get-tuple-element.282), channel_id=1, source_target_pairs={{0,24},{4,28},{8,0},{12,4},{16,8},{20,12},{24,16},{28,20},{1,25},{... | collective-permute-start | bytes 2359304 | tf_op jit(solution)/shard_map/cond/branch_5_fun/ppermute | solution.py:493
  9.9 60.7 %collective-permute-start.23 = (bf16[12,32,1024]{2,1,0:T(8,128)(2,1)S(1)}, bf16[12,32,1024]{2,1,0:T(8,128)(2,1)}, u32[]{:S(2)}, u32[]{:S(2)}) collective-permute-start(bf16[12,32,1024]{2,1,0:T(8,128)(2,1)S(1)} %get-tuple-element.283), channel_id=1, source_target_pairs={{0,24},{4,28},{8,0},{12,4},{16,8},{20,12},{24,16},{28,20},{1,25},{... | collective-permute-start | bytes 2359304 | tf_op jit(solution)/shard_map/cond/branch_5_fun/ppermute | solution.py:494
  10.1 33.6 %collective-permute-start.20 = (bf16[1,2560]{1,0:T(2,128)(2,1)S(1)}, bf16[1,2560]{1,0:T(2,128)(2,1)S(1)}, u32[]{:S(2)}, u32[]{:S(2)}) collective-permute-start(bf16[1,2560]{1,0:T(2,128)(2,1)S(1)} %get-tuple-element.272), channel_id=1, source_target_pairs={{0,8},{4,12},{8,16},{12,20},{16,24},{20,28},{24,0},{28,4},{1,9},{5... | collective-permute-start | bytes 15368 | tf_op jit(solution)/shard_map/cond/branch_5_fun/ppermute | solution.py:492
  66.2 4.4 %collective-permute-start.21 = (bf16[1,2048]{1,0:T(2,128)(2,1)S(1)}, bf16[1,2048]{1,0:T(2,128)(2,1)}, u32[]{:S(2)}, u32[]{:S(2)}) collective-permute-start(bf16[1,2048]{1,0:T(2,128)(2,1)S(1)} %get-tuple-element.281), channel_id=1, source_target_pairs={{0,24},{4,28},{8,0},{12,4},{16,8},{20,12},{24,16},{28,20},{1,25},{... | collective-permute-start | bytes 12296 | tf_op jit(solution)/shard_map/cond/branch_5_fun/ppermute | solution.py:506
